TPU v7x, 32 devices: a whole 2x2x4 slice. The times are simulated.
32 devices in a mesh: tile: 8 (over z, x), mem: 4 (over y, core).
Axes of the slice: x: 2, y: 2, z: 4, core: 2. Of those that a mesh axis runs over, the one named last changes fastest.
Arguments:
- footprints: bfloat16 [1024, 128, 128], P('tile'), may hold values from -0.1875 to 0.1875
- tile_row: int32 [1024], P('tile'), may hold values from 0 to 127, as said below
- tile_col: int32 [1024], P('tile'), may hold values from 0 to 63, as said below
- prior_flux: bfloat16 [256, 8192], P('mem', 'tile'), may hold values from -12 to 12
- observed: float32 [256, 16384], P('mem', 'tile'), may hold values from -6 to 6
- precision_weight: int32 [16384], P('tile'), may hold values from 1 to 16
Outputs:
- gradient: float32 [256, 8192], P('mem', 'tile')
Inputs may be any that keep to these rules, and one draw needn't show every extreme that they name: Among the 128 tiles of each index of tile, at most 24 have a row block of one owner (owner = tile_row // 16); in every draw one owner gets exactly 24 from every index. Likewise with owner = tile_col // 8: at most 24 from one index of tile to one owner, and one owner gets exactly 24 from every index.
All inputs are finite; a program needn't handle non-finite values.
Results may differ from a plain program's by a relative error of at most 0.0052.
Values may be sent and summed in bfloat16 or wider, within the bound.
No kernel may reach another device: no remote copies, remote signals or barrier semaphores. Data moves between devices by JAX's collectives and lax.ppermute only.
A program may use at most 64 MiB of HBM per device.

v0:
```python
import jax
import jax.numpy as jnp
from jax import lax
from jax.sharding import PartitionSpec as P

MEMBERS = 256
FLUX_DEV = 8
SOUND_DEV = 16


def slot_of(owners, capacity):
    entries = owners.shape[0]
    position = jnp.arange(entries)
    earlier = (owners[:, None] == owners[None, :]) & (position[None, :] < position[:, None])
    return owners * capacity + jnp.sum(earlier.astype(jnp.int32), axis=1)


def invert(slot_ids, slot_total):
    matches = slot_ids[None, :] == jnp.arange(slot_total)[:, None]
    sources = jnp.sum(jnp.where(matches, jnp.arange(slot_ids.shape[0])[None, :], 0), axis=1)
    return (sources, jnp.any(matches, axis=1))


def to_slots(values, sources, usage_flags):
    placed = jnp.take(values, sources, axis=1)
    return jnp.where(usage_flags[None, :, None], placed, jnp.zeros_like(placed))


def body(footprints, tile_row, tile_col, prior_flux, observed, precision_weight):
    devices_tile = lax.axis_size("tile")
    tile_count = footprints.shape[0]
    tile_size = footprints.shape[1]
    capacity = tile_count // devices_tile + max(1, tile_count // (2 * devices_tile))
    slot_total = devices_tile * capacity
    local_members = prior_flux.shape[0]
    local_sum = jnp.sum(prior_flux.astype(jnp.float32), axis=0)
    ensemble_sum = lax.psum(local_sum, "mem")
    ensemble_mean = ensemble_sum / MEMBERS
    member_deviations = (prior_flux.astype(jnp.float32) - ensemble_mean[None, :]).astype(
        jnp.bfloat16
    )
    row_owner = tile_row // SOUND_DEV
    row_local = tile_row % SOUND_DEV
    row_slot = slot_of(row_owner, capacity)
    row_source, row_used = invert(row_slot, slot_total)
    gathered = lax.all_gather(member_deviations, "tile", axis=1, tiled=True)
    retrieved_blocks = jnp.take(gathered.reshape(local_members, -1, tile_size), tile_col, axis=1)
    forward_terms = jnp.einsum(
        "mtk,trk->mtr", retrieved_blocks, footprints, preferred_element_type=jnp.float32
    )
    row_index = jnp.where(row_used, jnp.take(row_local, row_source), SOUND_DEV)
    sent_terms = to_slots(forward_terms, row_source, row_used)
    got_terms, got_rows = (
        lax.all_to_all(sent_terms, "tile", split_axis=1, concat_axis=1, tiled=True),
        lax.all_to_all(row_index[None, :], "tile", split_axis=1, concat_axis=1, tiled=True),
    )
    got_rows = got_rows[0]
    row_match = (got_rows[None, :] == jnp.arange(SOUND_DEV)[:, None]).astype(jnp.float32)
    modelled = jnp.einsum("ds,msk->mdk", row_match, got_terms, precision=lax.Precision.HIGHEST)
    targets = observed.reshape(local_members, SOUND_DEV, tile_size)
    obs_weight = (precision_weight.astype(jnp.float32) / 8.0).reshape(SOUND_DEV, tile_size)
    weighted = (obs_weight[None, :, :] * (modelled - targets)).astype(jnp.bfloat16)
    reply_rows = jnp.take(weighted, jnp.minimum(got_rows, SOUND_DEV - 1), axis=1)
    returned = lax.all_to_all(reply_rows, "tile", split_axis=1, concat_axis=1, tiled=True)
    residual_tiles = jnp.take(returned, row_slot, axis=1)
    backward_terms = jnp.einsum(
        "mtr,trk->mtk", residual_tiles, footprints, preferred_element_type=jnp.float32
    )
    picked = (tile_col[None, :] == jnp.arange(lax.axis_size("tile") * FLUX_DEV)[:, None]).astype(
        jnp.float32
    )
    reduced_total = lax.psum_scatter(
        jnp.einsum("ct,mtk->cmk", picked, backward_terms, precision=lax.Precision.HIGHEST),
        "tile",
        scatter_dimension=0,
        tiled=True,
    )
    gradient = reduced_total.transpose(1, 0, 2).reshape(local_members, FLUX_DEV * tile_size)
    return gradient


def solution(mesh):
    in_specs = (
        P("tile", None, None),
        P("tile"),
        P("tile"),
        P("mem", "tile"),
        P("mem", "tile"),
        P("tile"),
    )
    out_specs = P("mem", "tile")
    return jax.shard_map(body, mesh=mesh, in_specs=in_specs, out_specs=out_specs, check_vma=False)
```

profile of v0, /device:TPU:0, one launch (start us, length us, event | category | flops | bytes accessed | tf_op | source)
XLA Modules:
  0.0 394.9 jit_solution(9114734959783431947)
XLA Ops:
  6.5 0.9 convert_reduce_fusion
  7.5 8.4 %psum.7 = f32[1024]{0:T(1024)S(1)} all-reduce(f32[1024]{0:T(1024)S(1)} %convert_reduce_fusion), channel_id=1, replica_groups=mesh['tile'=8,'mem'=4] {'mem'}, use_global_device_ids=true, to_apply=%region_4.5 | all-reduce | flops 1024 | bytes 8192 | tf_op jit(solution)/shard_map/psum | solution.py:37
  15.9 1.6 fusion.24
  18.6 1.6 gather_fusion
  21.0 5.8 %all-to-all-start = ((s32[1,8,24]{2,0,1:T(1,128)}), s32[1,8,24]{2,0,1:T(1,128)S(1)}, u32[]{:S(2)}, u32[]{:S(2)}) async-start(s32[1,8,24]{2,0,1:T(1,128)} %bitcast.3), calls=%async_computation | async-start | bytes 8192 | tf_op jit(solution)/shard_map/all_to_all | solution.py:55
  28.2 30.0 %all-gather.2.cloned.1.call-done = bf16[64,8192]{1,0:T(8,128)(2,1)} async-done(((bf16[64,1024]{1,0:T(8,128)(2,1)}), bf16[64,8192]{1,0:T(8,128)(2,1)}) %all-gather.2.cloned.1.call-update) | async-done | bytes 1048592 | tf_op jit(solution)/shard_map/all_gather | solution.py:46
  58.2 1.5 copy_bitcast_fusion
  59.7 1.0 gather_fusion.1
  60.7 7.0 %convolution_bitcast_fusion.1 = f32[64,128,128]{2,0,1:T(8,128)} fusion(bf16[128,128,128]{2,1,0:T(8,128)(2,1)} %param.6, bf16[128,64,128]{2,1,0:T(8,128)(2,1)S(1)} %gather_fusion.1, pred[128]{0:T(512)(128)(4,1)S(1)} %compare_and_fusion), kind=kOutput, calls=%fused_computation.12 | convolution fusion | flops 269484032 | bytes 10485888 | tf_op jit(solution)/shard_map/mtk,trk->mtr/dot_general | solution.py:48
  67.7 5.8 %gather_fusion.2 = f32[192,64,128]{2,1,0:T(8,128)} fusion(f32[64,128,128]{2,0,1:T(8,128)} %convolution_bitcast_fusion.1, s32[1024]{0:T(1024)S(1)} %pad_clamp_fusion.3), kind=kCustom, calls=%fused_computation.2 | custom fusion | bytes 12583680 | tf_op jit(solution)/shard_map/jit(_take)/gather | solution.py:25
  73.5 5.4 %select_bitcast_fusion = f32[64,192,128]{2,0,1:T(8,128)} fusion(f32[192,64,128]{2,1,0:T(8,128)} %gather_fusion.2, pred[192]{0:T(512)(128)(4,1)S(1)} %fusion.25, pred[192]{0:T(512)(128)(4,1)S(1)} %compare_and_fusion.1), kind=kLoop, calls=%fused_computation.7 | loop fusion | flops 3145728 | bytes 12583296 | tf_op jit(solution)/shard_map/jit(_where)/select_n | solution.py:26
  79.0 4.9 %all-to-all-start.1 = ((f32[64,192,128]{2,0,1:T(8,128)}), f32[64,192,128]{2,0,1:T(8,128)}, u32[]{:S(2)}, u32[]{:S(2)}) async-start(f32[64,192,128]{2,0,1:T(8,128)} %select_bitcast_fusion), calls=%async_computation.1 | async-start | bytes 12582912 | tf_op jit(solution)/shard_map/all_to_all | solution.py:54
  84.5 0.7 minimum_reduce_fusion
  85.4 135.2 %all-to-all-done.1 = f32[64,192,128]{2,0,1:T(8,128)} async-done(((f32[64,192,128]{2,0,1:T(8,128)}), f32[64,192,128]{2,0,1:T(8,128)}, u32[]{:S(2)}, u32[]{:S(2)}) %all-to-all-start.1) | async-done | bytes 6291488 | tf_op jit(solution)/shard_map/all_to_all | solution.py:54
  220.6 8.1 %fusion.19 = bf16[64,16,128]{2,1,0:T(8,128)(2,1)S(1)} fusion(f32[64,16,128]{2,1,0:T(8,128)S(1)} %bitcast.49, f32[64,192,128]{2,0,1:T(8,128)} %all-to-all-done.1, f32[16,128]{1,0:T(8,128)S(1)} %multiply_bitcast_fusion, s32[192]{0:T(256)S(1)} %squeeze.3), kind=kOutput, calls=%fused_computation.22 | convolution fusion | flops 302386176 | bytes 7086848 | tf_op jit(solution)/shard_map/ds,msk->mdk/dot_general | solution.py:59
  228.7 1.2 gather_fusion.3
  229.9 2.1 select_bitcast_fusion.1
  232.0 3.6 all-to-all-start.2
  235.7 70.8 %all-to-all-done.2 = bf16[64,192,128]{2,0,1:T(8,128)(2,1)S(1)} async-done(((bf16[64,192,128]{2,0,1:T(8,128)(2,1)}), bf16[64,192,128]{2,0,1:T(8,128)(2,1)S(1)}, u32[]{:S(2)}, u32[]{:S(2)}) %all-to-all-start.2) | async-done | bytes 3145760 | tf_op jit(solution)/shard_map/all_to_all | solution.py:64
  306.5 2.2 gather_fusion.4
  308.7 4.1 %convolution_bitcast_fusion = f32[64,128,128]{2,0,1:T(8,128)S(1)} fusion(bf16[128,128,128]{2,1,0:T(8,128)(2,1)} %param.6, bf16[128,64,128]{2,1,0:T(8,128)(2,1)} %gather_fusion.4, pred[128]{0:T(512)(128)(4,1)S(1)} %get-tuple-element.7), kind=kOutput, calls=%fused_computation.11 | convolution fusion | flops 269484032 | bytes 10485888 | tf_op jit(solution)/shard_map/mtr,trk->mtk/dot_general | solution.py:66
  312.8 5.4 %fusion.2 = f32[64,64,128]{2,0,1:T(8,128)} fusion(f32[64,128,128]{2,0,1:T(8,128)S(1)} %convolution_bitcast_fusion, s32[128]{0:T(128)S(1)} %copy-done.2), kind=kOutput, calls=%fused_computation.8 | convolution fusion | flops 805314560 | bytes 6291968 | tf_op jit(solution)/shard_map/ct,mtk->cmk/dot_general | solution.py:73
  318.3 68.2 %reduce-scatter.2.cloned.1.call-done = f32[8,64,128]{2,0,1:T(8,128)} async-done(((f32[64,64,128]{2,0,1:T(8,128)}), f32[8,64,128]{2,0,1:T(8,128)}) %reduce-scatter.2.cloned.1.call-update) | async-done | bytes 262160 | tf_op jit(solution)/shard_map/reduce_scatter | solution.py:72
  386.4 1.7 copy.42
  (38 shorter events, 4.3 us)
Async XLA Ops:
  6.5 51.7 %all-gather.2.cloned.1.call-start = ((), (), s32[]{:S(2)}) async-start(), calls=%async_computation.4 | async-start | bytes 1179648 | tf_op jit(solution)/shard_map/all_gather | solution.py:46
  21.0 57.9 %all-to-all-start = ((s32[1,8,24]{2,0,1:T(1,128)}), s32[1,8,24]{2,0,1:T(1,128)S(1)}, u32[]{:S(2)}, u32[]{:S(2)}) async-start(s32[1,8,24]{2,0,1:T(1,128)} %bitcast.3), calls=%async_computation | async-start | bytes 8192 | tf_op jit(solution)/shard_map/all_to_all | solution.py:55
  79.0 4.9 %copy-start = (f32[64,2048]{1,0:T(8,128)S(1)}, f32[64,2048]{1,0:T(8,128)}, u32[]{:S(2)}) copy-start(f32[64,2048]{1,0:T(8,128)} %param.10) | copy-start | bytes 1572868
  79.0 5.0 %copy-start.1 = (s32[2048]{0:T(1024)S(1)}, s32[2048]{0:T(1024)}, u32[]{:S(2)}) copy-start(s32[2048]{0:T(1024)} %param.11) | copy-start | bytes 24580
  79.0 141.6 %all-to-all-start.1 = ((f32[64,192,128]{2,0,1:T(8,128)}), f32[64,192,128]{2,0,1:T(8,128)}, u32[]{:S(2)}, u32[]{:S(2)}) async-start(f32[64,192,128]{2,0,1:T(8,128)} %select_bitcast_fusion), calls=%async_computation.1 | async-start | bytes 12582912 | tf_op jit(solution)/shard_map/all_to_all | solution.py:54
  232.0 74.5 %all-to-all-start.2 = ((bf16[64,192,128]{2,0,1:T(8,128)(2,1)}), bf16[64,192,128]{2,0,1:T(8,128)(2,1)S(1)}, u32[]{:S(2)}, u32[]{:S(2)}) async-start(bf16[64,192,128]{2,0,1:T(8,128)(2,1)} %select_bitcast_fusion.1), calls=%async_computation.2 | async-start | bytes 6291456 | tf_op jit(solution)/shard_map/all_to_all | solution.py:64
  235.6 150.8 %reduce-scatter.2.cloned.1.call-start = ((), (), s32[]{:S(2)}) async-start(), calls=%async_computation.5 | async-start | bytes 2359296 | tf_op jit(solution)/shard_map/reduce_scatter | solution.py:72
  308.7 4.1 %copy-start.2 = (s32[128]{0:T(128)S(1)}, s32[128]{0:T(128)}, u32[]{:S(2)}) copy-start(s32[128]{0:T(128)} %param.8) | copy-start | bytes 1540
Sparse Core Ops, SparseCore 0:
  17.6 40.5 all-gather.1
  318.4 67.9 reduce-scatter.1
where the time goes:
time: 396 us; the launch traced here: 395 us
  waiting for transfers between devices  304 us (77%)
  matrix products  24.7 us (6%)
  local copies, waits for them, and re-layouts  15.9 us (4%)
  starting transfers between devices  14.4 us (4%)
  other arithmetic  13.8 us (3%)
  between operations  13.6 us (3%)
  blocking collectives  8.4 us (2%)
    all_to_all x1, waiting for transfers between devices, body(): lax.all_to_all(sent_terms, 'tile', split_axis=1, concat_axis=1, tiled=True)  135 us
    all_to_all x1, waiting for transfers between devices, body(): lax.all_to_all(reply_rows, 'tile', split_axis=1, concat_axis=1, tiled=True)  70.8 us
    reduce_scatter x1, waiting for transfers between devices, body(): lax.psum_scatter(jnp.einsum('ct,mtk->cmk', picked, backward_terms, precis...  68.2 us
    all_gather x1, waiting for transfers between devices, body(): gathered = lax.all_gather(member_deviations, 'tile', axis=1, tiled=True)  30 us
    psum x1, blocking collectives, body(): ensemble_sum = lax.psum(local_sum, 'mem')  8.4 us
    dot_general x1, matrix products, body(): jnp.einsum('ds,msk->mdk', row_match, got_terms, precision=lax.Precision.H...  8.12 us
  transfers between devices with their start and end apart: 5, of which 4 were waited for; matrix products, arithmetic and copies ran while one was open for 7% of the time, Pallas kernels for 0%

commit v1 on v0

--- a/solution.py
+++ b/solution.py
@@ -43,7 +43,8 @@
     row_local = tile_row % SOUND_DEV
     row_slot = slot_of(row_owner, capacity)
     row_source, row_used = invert(row_slot, slot_total)
-    gathered = lax.all_gather(member_deviations, "tile", axis=1, tiled=True)
+    parts = lax.all_gather(member_deviations, "tile", axis=0, tiled=False)
+    gathered = jnp.concatenate(parts, axis=1)
     retrieved_blocks = jnp.take(gathered.reshape(local_members, -1, tile_size), tile_col, axis=1)
     forward_terms = jnp.einsum(
         "mtk,trk->mtr", retrieved_blocks, footprints, preferred_element_type=jnp.float32

time: 396 us -> 397 us (level)
  no operation moved by 1% of the time
where the time goes in v1:
time: 397 us
  waiting for transfers between devices  304 us (77%)
  matrix products  24.7 us (6%)
  local copies, waits for them, and re-layouts  17.4 us (4%)
  starting transfers between devices  14.8 us (4%)
  other arithmetic  13.8 us (3%)
  between operations  13.6 us (3%)
  blocking collectives  8.4 us (2%)
    all_to_all x1, waiting for transfers between devices, body(): lax.all_to_all(sent_terms, 'tile', split_axis=1, concat_axis=1, tiled=True)  135 us
    all_to_all x1, waiting for transfers between devices, body(): lax.all_to_all(reply_rows, 'tile', split_axis=1, concat_axis=1, tiled=True)  70.6 us
    reduce_scatter x1, waiting for transfers between devices, body(): lax.psum_scatter(jnp.einsum('ct,mtk->cmk', picked, backward_terms, precis...  68.4 us
    all_gather x1, waiting for transfers between devices, body(): parts = lax.all_gather(member_deviations, 'tile', axis=0, tiled=False)  30.1 us
    psum x1, blocking collectives, body(): ensemble_sum = lax.psum(local_sum, 'mem')  8.4 us
    dot_general x1, matrix products, body(): jnp.einsum('ds,msk->mdk', row_match, got_terms, precision=lax.Precision.H...  8.12 us
  transfers between devices with their start and end apart: 5, of which 4 were waited for; matrix products, arithmetic and copies ran while one was open for 7% of the time, Pallas kernels for 0%

profile of v1, /device:TPU:0, one launch (start us, length us, event | category | flops | bytes accessed | tf_op | source)
XLA Modules:
  0.0 396.7 jit_solution(2656614828763084823)
XLA Ops:
  6.5 0.9 convert_reduce_fusion
  7.5 8.4 %psum.7 = f32[1024]{0:T(1024)S(1)} all-reduce(f32[1024]{0:T(1024)S(1)} %convert_reduce_fusion), channel_id=1, replica_groups=mesh['tile'=8,'mem'=4] {'mem'}, use_global_device_ids=true, to_apply=%region_4.5 | all-reduce | flops 1024 | bytes 8192 | tf_op jit(solution)/shard_map/psum | solution.py:37
  15.9 1.6 fusion.24
  18.6 1.6 gather_fusion
  21.0 5.8 %all-to-all-start = ((s32[1,8,24]{2,0,1:T(1,128)}), s32[1,8,24]{2,0,1:T(1,128)S(1)}, u32[]{:S(2)}, u32[]{:S(2)}) async-start(s32[1,8,24]{2,0,1:T(1,128)} %bitcast.3), calls=%async_computation | async-start | bytes 8192 | tf_op jit(solution)/shard_map/all_to_all | solution.py:56
  28.2 30.1 %all-gather.3.cloned.1.call-done = bf16[512,1024]{1,0:T(8,128)(2,1)} async-done(((bf16[64,1024]{1,0:T(8,128)(2,1)}), bf16[512,1024]{1,0:T(8,128)(2,1)}) %all-gather.3.cloned.1.call-update) | async-done | bytes 1048592 | tf_op jit(solution)/shard_map/all_gather | solution.py:46
  58.2 1.8 copy.47
  60.5 0.7 copy.27
  61.2 1.0 gather_fusion.1
  62.2 7.0 %convolution_bitcast_fusion.1 = f32[64,128,128]{2,0,1:T(8,128)} fusion(bf16[128,128,128]{2,1,0:T(8,128)(2,1)} %param.6, bf16[128,64,128]{2,1,0:T(8,128)(2,1)S(1)} %gather_fusion.1, pred[128]{0:T(512)(128)(4,1)S(1)} %compare_and_fusion), kind=kOutput, calls=%fused_computation.12 | convolution fusion | flops 269484032 | bytes 10485888 | tf_op jit(solution)/shard_map/mtk,trk->mtr/dot_general | solution.py:49
  69.2 5.8 %gather_fusion.2 = f32[192,64,128]{2,1,0:T(8,128)} fusion(f32[64,128,128]{2,0,1:T(8,128)} %convolution_bitcast_fusion.1, s32[1024]{0:T(1024)S(1)} %pad_clamp_fusion.3), kind=kCustom, calls=%fused_computation.2 | custom fusion | bytes 12583680 | tf_op jit(solution)/shard_map/jit(_take)/gather | solution.py:25
  75.0 5.4 %select_bitcast_fusion = f32[64,192,128]{2,0,1:T(8,128)} fusion(f32[192,64,128]{2,1,0:T(8,128)} %gather_fusion.2, pred[192]{0:T(512)(128)(4,1)S(1)} %fusion.25, pred[192]{0:T(512)(128)(4,1)S(1)} %compare_and_fusion.1), kind=kLoop, calls=%fused_computation.7 | loop fusion | flops 3145728 | bytes 12583296 | tf_op jit(solution)/shard_map/jit(_where)/select_n | solution.py:26
  80.5 5.1 %all-to-all-start.1 = ((f32[64,192,128]{2,0,1:T(8,128)}), f32[64,192,128]{2,0,1:T(8,128)}, u32[]{:S(2)}, u32[]{:S(2)}) async-start(f32[64,192,128]{2,0,1:T(8,128)} %select_bitcast_fusion), calls=%async_computation.1 | async-start | bytes 12582912 | tf_op jit(solution)/shard_map/all_to_all | solution.py:55
  87.1 135.0 %all-to-all-done.1 = f32[64,192,128]{2,0,1:T(8,128)} async-done(((f32[64,192,128]{2,0,1:T(8,128)}), f32[64,192,128]{2,0,1:T(8,128)}, u32[]{:S(2)}, u32[]{:S(2)}) %all-to-all-start.1) | async-done | bytes 6291488 | tf_op jit(solution)/shard_map/all_to_all | solution.py:55
  222.1 8.1 %fusion.19 = bf16[64,16,128]{2,1,0:T(8,128)(2,1)S(1)} fusion(f32[64,16,128]{2,1,0:T(8,128)S(1)} %bitcast.49, f32[64,192,128]{2,0,1:T(8,128)} %all-to-all-done.1, f32[16,128]{1,0:T(8,128)S(1)} %multiply_bitcast_fusion, s32[192]{0:T(256)S(1)} %squeeze.3), kind=kOutput, calls=%fused_computation.22 | convolution fusion | flops 302386176 | bytes 7086848 | tf_op jit(solution)/shard_map/ds,msk->mdk/dot_general | solution.py:60
  230.2 1.2 gather_fusion.3
  231.4 2.1 select_bitcast_fusion.1
  233.5 3.6 all-to-all-start.2
  237.4 70.6 %all-to-all-done.2 = bf16[64,192,128]{2,0,1:T(8,128)(2,1)S(1)} async-done(((bf16[64,192,128]{2,0,1:T(8,128)(2,1)}), bf16[64,192,128]{2,0,1:T(8,128)(2,1)S(1)}, u32[]{:S(2)}, u32[]{:S(2)}) %all-to-all-start.2) | async-done | bytes 3145760 | tf_op jit(solution)/shard_map/all_to_all | solution.py:65
  308.0 2.2 gather_fusion.4
  310.2 4.1 %convolution_bitcast_fusion = f32[64,128,128]{2,0,1:T(8,128)S(1)} fusion(bf16[128,128,128]{2,1,0:T(8,128)(2,1)} %param.6, bf16[128,64,128]{2,1,0:T(8,128)(2,1)} %gather_fusion.4, pred[128]{0:T(512)(128)(4,1)S(1)} %get-tuple-element.7), kind=kOutput, calls=%fused_computation.11 | convolution fusion | flops 269484032 | bytes 10485888 | tf_op jit(solution)/shard_map/mtr,trk->mtk/dot_general | solution.py:67
  314.3 5.4 %fusion.2 = f32[64,64,128]{2,0,1:T(8,128)} fusion(f32[64,128,128]{2,0,1:T(8,128)S(1)} %convolution_bitcast_fusion, s32[128]{0:T(128)S(1)} %copy-done.2), kind=kOutput, calls=%fused_computation.8 | convolution fusion | flops 805314560 | bytes 6291968 | tf_op jit(solution)/shard_map/ct,mtk->cmk/dot_general | solution.py:74
  319.8 68.4 %reduce-scatter.2.cloned.1.call-done = f32[8,64,128]{2,0,1:T(8,128)} async-done(((f32[64,64,128]{2,0,1:T(8,128)}), f32[8,64,128]{2,0,1:T(8,128)}) %reduce-scatter.2.cloned.1.call-update) | async-done | bytes 262160 | tf_op jit(solution)/shard_map/reduce_scatter | solution.py:73
  388.2 1.7 copy.48
  (40 shorter events, 5.6 us)
Async XLA Ops:
  6.5 51.7 %all-gather.3.cloned.1.call-start = ((), (), s32[]{:S(2)}) async-start(), calls=%async_computation.5 | async-start | bytes 1179648 | tf_op jit(solution)/shard_map/all_gather | solution.py:46
  21.0 59.4 %all-to-all-start = ((s32[1,8,24]{2,0,1:T(1,128)}), s32[1,8,24]{2,0,1:T(1,128)S(1)}, u32[]{:S(2)}, u32[]{:S(2)}) async-start(s32[1,8,24]{2,0,1:T(1,128)} %bitcast.3), calls=%async_computation | async-start | bytes 8192 | tf_op jit(solution)/shard_map/all_to_all | solution.py:56
  80.5 5.1 %copy-start = (f32[64,2048]{1,0:T(8,128)S(1)}, f32[64,2048]{1,0:T(8,128)}, u32[]{:S(2)}) copy-start(f32[64,2048]{1,0:T(8,128)} %param.10) | copy-start | bytes 1572868
  80.5 5.2 %copy-start.1 = (s32[2048]{0:T(1024)S(1)}, s32[2048]{0:T(1024)}, u32[]{:S(2)}) copy-start(s32[2048]{0:T(1024)} %param.11) | copy-start | bytes 24580
  80.5 141.6 %all-to-all-start.1 = ((f32[64,192,128]{2,0,1:T(8,128)}), f32[64,192,128]{2,0,1:T(8,128)}, u32[]{:S(2)}, u32[]{:S(2)}) async-start(f32[64,192,128]{2,0,1:T(8,128)} %select_bitcast_fusion), calls=%async_computation.1 | async-start | bytes 12582912 | tf_op jit(solution)/shard_map/all_to_all | solution.py:55
  233.5 74.5 %all-to-all-start.2 = ((bf16[64,192,128]{2,0,1:T(8,128)(2,1)}), bf16[64,192,128]{2,0,1:T(8,128)(2,1)S(1)}, u32[]{:S(2)}, u32[]{:S(2)}) async-start(bf16[64,192,128]{2,0,1:T(8,128)(2,1)} %select_bitcast_fusion.1), calls=%async_computation.2 | async-start | bytes 6291456 | tf_op jit(solution)/shard_map/all_to_all | solution.py:65
  237.1 151.0 %reduce-scatter.2.cloned.1.call-start = ((), (), s32[]{:S(2)}) async-start(), calls=%async_computation.4 | async-start | bytes 2359296 | tf_op jit(solution)/shard_map/reduce_scatter | solution.py:73
  310.2 4.1 %copy-start.2 = (s32[128]{0:T(128)S(1)}, s32[128]{0:T(128)}, u32[]{:S(2)}) copy-start(s32[128]{0:T(128)} %param.8) | copy-start | bytes 1540
Sparse Core Ops, SparseCore 0:
  17.6 40.5 all-gather.2
  319.9 68.2 reduce-scatter.1
